TPU v7x, 32 devices: a whole 2x2x4 slice. The times are simulated.
32 devices in a mesh: batch: 4 (over z), seq: 4 (over y, core), head: 2 (over x).
Axes of the slice: x: 2, y: 2, z: 4, core: 2. Of those that a mesh axis runs over, the one named last changes fastest.
Arguments:
- image_hidden: bfloat16 [8, 1024, 3072], P('batch', 'seq', 'head'), parts along dimension 0, may hold values from -6 to 6
- modulation: float32 [8, 3, 3072], P('batch'), parts along dimension 0, may hold values from -4 to 4
- qkv_weight: bfloat16 [3072, 3, 1536], P(None, None, 'head'), may hold values from -0.109375 to 0.109375
- out_weight: bfloat16 [1536, 3072], P('head'), may hold values from -0.15625 to 0.15625
- q_gain: float32 [128], replicated, may hold values from 1.2 to 2.5
- k_gain: float32 [128], replicated, may hold values from 1.2 to 2.5
- text_keys: bfloat16 [8, 128, 1536], P('batch', 'seq', 'head'), parts along dimension 0, may hold values from -10 to 10
- text_values: bfloat16 [8, 128, 1536], P('batch', 'seq', 'head'), parts along dimension 0, may hold values from -6 to 6
- stale_keys: bfloat16 [8, 1024, 1536], P('batch', 'seq', 'head'), parts along dimension 0, may hold values from -64 to 64
- stale_values: bfloat16 [8, 1024, 1536], P('batch', 'seq', 'head'), parts along dimension 0, may hold values from -6 to 6
- cached_residual: bfloat16 [8, 1024, 3072], P('batch', 'seq', 'head'), parts along dimension 0, may hold values from -6 to 6
- patch_of: int32 [16], P('batch'), parts along dimension 0, may hold values from 0 to 3, each once
- refresh: int32 [16], P('batch'), parts along dimension 0, may hold values from 0 to 1, as said below
- text_len: int32 [8], P('batch'), parts along dimension 0, may hold values from 16 to 128
Outputs:
- image_out: bfloat16 [8, 1024, 3072], P('batch', 'seq', 'head'), parts along dimension 0
There are 4 independent parts, one for each index of `batch`. A program takes and returns all parts, laid end to end along the dimension named above; an argument that names none is the same for every part. Nothing has to cross between parts.
Inputs may be any that keep to these rules, and one draw needn't show every extreme that they name: `patch_of`: A permutation: every image band sits on exactly one index of seq. `refresh`: exactly 1 entries are 1, the rest 0.
All inputs are finite; a program needn't handle non-finite values.
Results may differ from a plain program's by a relative error of at most 0.012.
The roundings to bfloat16 on the way count: a program that leaves them out, or rounds other values in their place, can miss the bound.
Values may be sent and summed in bfloat16 or wider, within the bound.
A program may use at most 192 MiB of HBM per device.

v0:
```python
import jax
import jax.numpy as jnp
from jax import lax
from jax.sharding import PartitionSpec as P

GRID_W = 64
epsilon = 1e-06


def rotary_tables(raster, head_dim, grid_width):
    half_dim = head_dim // 2
    first_pairs = head_dim // 16
    axis_pairs = (half_dim - first_pairs) // 2
    pair_index = jnp.arange(half_dim, dtype=jnp.int32)
    pair_local = jnp.where(
        pair_index < first_pairs + axis_pairs,
        pair_index - first_pairs,
        pair_index - first_pairs - axis_pairs,
    )
    exponent = -pair_local.astype(jnp.float32) / float(axis_pairs)
    frequency = jnp.where(
        pair_index < first_pairs, jnp.float32(0.0), jnp.power(jnp.float32(10000.0), exponent)
    )
    row_pos = (raster // grid_width).astype(jnp.float32)
    col_pos = (raster % grid_width).astype(jnp.float32)
    position = jnp.where(
        pair_index[None, :] < first_pairs + axis_pairs, row_pos[:, None], col_pos[:, None]
    )
    angles = position * frequency[None, :]
    cosine = jnp.cos(angles)
    sine = jnp.sin(angles)
    return (jnp.concatenate([cosine, cosine], axis=-1), jnp.concatenate([-sine, sine], axis=-1))


def rms_rotate(vectors, gain_vec, cos_full, sin_full):
    scaled = (
        vectors
        * lax.rsqrt(jnp.mean(vectors * vectors, axis=-1, keepdims=True) + epsilon)
        * gain_vec
    )
    half_dim = vectors.shape[-1] // 2
    return (
        scaled * cos_full[None, :, None, :]
        + jnp.roll(scaled, half_dim, axis=-1) * sin_full[None, :, None, :]
    )


def per_device(
    image_hidden,
    modulation,
    qkv_weight,
    out_weight,
    q_gain,
    k_gain,
    text_keys,
    text_values,
    stale_keys,
    stale_values,
    cached_residual,
    patch_of,
    refresh,
    text_len,
):
    prompts, tok_rows, width_part = image_hidden.shape
    head_dim = q_gain.shape[0]
    channels = out_weight.shape[0]
    local_heads = channels // head_dim
    seq_seat = lax.axis_index("seq")
    head_seat = lax.axis_index("head")
    gathered = lax.all_gather(image_hidden, "head", axis=2, tiled=True)
    model_width = gathered.shape[2]
    hidden_f32 = gathered.astype(jnp.float32)
    row_mean = jnp.mean(hidden_f32, axis=-1, keepdims=True)
    centered = hidden_f32 - row_mean
    variance = jnp.mean(centered * centered, axis=-1, keepdims=True)
    normed = centered * lax.rsqrt(variance + epsilon)
    modulated = (
        normed * (1.0 + modulation[:, 1][:, None, :]) + modulation[:, 0][:, None, :]
    ).astype(jnp.bfloat16)
    projected = jnp.dot(
        modulated.reshape(prompts * tok_rows, model_width),
        qkv_weight.reshape(model_width, 3 * channels),
        preferred_element_type=jnp.float32,
    )
    projected = projected.reshape(prompts, tok_rows, 3, local_heads, head_dim)
    seat_ids = jnp.arange(patch_of.shape[0], dtype=jnp.int32)
    own_band = jnp.sum(jnp.where(seat_ids == seq_seat, patch_of, 0))
    own_flag = jnp.sum(jnp.where(seat_ids == seq_seat, refresh, 0))
    raster = own_band * tok_rows + jnp.arange(tok_rows, dtype=jnp.int32)
    cos_full, sin_full = rotary_tables(raster, head_dim, GRID_W)
    fresh_q = rms_rotate(projected[:, :, 0], q_gain, cos_full, sin_full).astype(jnp.bfloat16)
    fresh_k = rms_rotate(projected[:, :, 1], k_gain, cos_full, sin_full).astype(jnp.bfloat16)
    fresh_v = projected[:, :, 2].astype(jnp.bfloat16)
    fresh_k_flat = fresh_k.reshape(prompts, tok_rows, channels)
    fresh_v_flat = fresh_v.reshape(prompts, tok_rows, channels)
    score_scale = head_dim ** (-0.5)
    text_k, text_v = (
        lax.all_gather(text_keys, "seq", axis=1, tiled=True),
        lax.all_gather(text_values, "seq", axis=1, tiled=True),
    )
    total_text = text_k.shape[1]
    text_key_rows = text_k.reshape(prompts, total_text, local_heads, head_dim)
    text_value_rows = text_v.reshape(prompts, total_text, local_heads, head_dim)
    text_scores = (
        jnp.einsum("pqhd,pkhd->phqk", fresh_q, text_key_rows, preferred_element_type=jnp.float32)
        * score_scale
    )
    text_valid = jnp.arange(total_text, dtype=jnp.int32)[None, :] < text_len[:, None]
    text_scores = jnp.where(text_valid[:, None, None, :], text_scores, -1e30)
    row_top = jnp.max(text_scores, axis=-1)
    text_weights = jnp.exp(text_scores - row_top[..., None])
    row_total = jnp.sum(text_weights, axis=-1)
    weighted = jnp.einsum(
        "phqk,pkhd->phqd",
        text_weights.astype(jnp.bfloat16),
        text_value_rows,
        preferred_element_type=jnp.float32,
    )
    running = (row_top, row_total, weighted)
    chosen_k = jnp.where(own_flag == 1, fresh_k_flat, stale_keys)
    chosen_v = jnp.where(own_flag == 1, fresh_v_flat, stale_values)
    key_rows = lax.all_gather(chosen_k[None], "seq", axis=0, tiled=True)
    value_rows = lax.all_gather(chosen_v[None], "seq", axis=0, tiled=True)
    piece_count = key_rows.shape[0]
    is_mine = jnp.arange(piece_count, dtype=jnp.int32) == seq_seat
    key_rows = jnp.where(is_mine[:, None, None, None], fresh_k_flat[None], key_rows)
    value_rows = jnp.where(is_mine[:, None, None, None], fresh_v_flat[None], value_rows)
    key_rows = key_rows.reshape(piece_count, prompts, tok_rows, local_heads, head_dim)
    value_rows = value_rows.reshape(piece_count, prompts, tok_rows, local_heads, head_dim)
    old_top, old_total, old_weighted = running
    scores = (
        jnp.einsum("pqhd,npkhd->phqnk", fresh_q, key_rows, preferred_element_type=jnp.float32)
        * score_scale
    )
    new_top = jnp.maximum(old_top, jnp.max(scores, axis=(3, 4)))
    shrink = jnp.exp(old_top - new_top)
    weights = jnp.exp(scores - new_top[..., None, None])
    new_total = old_total * shrink + jnp.sum(weights, axis=(3, 4))
    added = jnp.einsum(
        "phqnk,npkhd->phqd",
        weights.astype(jnp.bfloat16),
        value_rows,
        preferred_element_type=jnp.float32,
    )
    running = (new_top, new_total, old_weighted * shrink[..., None] + added)
    final_top, final_total, final_weighted = running
    attended = (final_weighted / final_total[..., None]).astype(jnp.bfloat16)
    partial_value = jnp.einsum(
        "phqd,hde->pqe",
        attended,
        out_weight.reshape(local_heads, head_dim, model_width),
        preferred_element_type=jnp.float32,
    )
    reduced = lax.psum_scatter(
        partial_value.astype(jnp.bfloat16), "head", scatter_dimension=2, tiled=True
    ).astype(jnp.float32)
    gate_part = lax.dynamic_slice_in_dim(modulation[:, 2], head_seat * width_part, width_part, 1)
    result = (
        image_hidden.astype(jnp.float32)
        + gate_part[:, None, :] * reduced
        + cached_residual.astype(jnp.float32)
    )
    return result.astype(jnp.bfloat16)


def solution(mesh):
    in_specs = (
        P("batch", "seq", "head"),
        P("batch", None, None),
        P(None, None, "head"),
        P("head", None),
        P(),
        P(),
        P("batch", "seq", "head"),
        P("batch", "seq", "head"),
        P("batch", "seq", "head"),
        P("batch", "seq", "head"),
        P("batch", "seq", "head"),
        P("batch"),
        P("batch"),
        P("batch"),
    )
    out_specs = P("batch", "seq", "head")
    return jax.shard_map(
        per_device, mesh=mesh, in_specs=in_specs, out_specs=out_specs, check_vma=False
    )
```

profile of v0, /device:TPU:0, one launch (start us, length us, event | category | flops | bytes accessed | tf_op | source)
XLA Modules:
  0.0 229.3 jit_solution(13103266877624958867)
XLA Ops:
  6.5 0.7 all-gather.6.cloned.1.call-update
  7.3 18.8 %copy.40 = bf16[3072,3,768]{0,2,1:T(8,128)(2,1)} copy(bf16[3072,3,768]{2,0,1:T(8,128)(2,1)} %param.16) | data formatting | bytes 28311552 | tf_op args[2]
  26.1 0.7 select_reduce_fusion
  27.5 0.3 fusion.45
  27.9 0.6 copy-done.9
  28.6 1.2 copy.52
  29.8 0.7 copy-done.11
  30.5 1.2 copy.51
  32.4 0.6 fusion.59
  33.0 23.5 %all-gather.6.cloned.1.call-done = bf16[2,256,3072]{2,1,0:T(8,128)(2,1)} async-done(((bf16[2,256,1536]{2,1,0:T(8,128)(2,1)}), bf16[2,256,3072]{2,1,0:T(8,128)(2,1)}) %all-gather.6.cloned.1.call-update) | async-done | bytes 3145744 | tf_op jit(solution)/shard_map/all_gather | solution.py:70
  56.5 2.5 %convert_reduce_fusion = f32[2,256]{1,0:T(2,128)S(1)} fusion(bf16[2,256,3072]{2,1,0:T(8,128)(2,1)} %all-gather.6.cloned.1.call-done), kind=kLoop, calls=%fused_computation.5 | loop fusion | flops 3145216 | bytes 3147776 | tf_op jit(solution)/shard_map/reduce_sum | solution.py:73
  59.1 0.3 copy-done.2
  59.4 1.0 fusion.4
  60.3 10.8 %fusion.13 = f32[2,256,3,6,128]{1,4,3,2,0:T(8,128)S(1)} fusion(bf16[3,6,128,3072,1]{3,2,1,0,4:T(8,128)(2,1)} %bitcast.73, bf16[2,256,3072]{2,1,0:T(8,128)(2,1)S(1)} %copy-done.2, f32[2,3072]{1,0:T(2,128)S(1)} %get-tuple-element.18, f32[2,3072]{1,0:T(2,128)S(1)} %get-tuple-element.19, f32[2,256]{1,0:T(2,128)S(1)} %add_rsqrt_fusion.2, ...), kind=kOutput, calls=%fused_computation.17 | convolution fusion | flops 7257194496 | bytes 22073344 | tf_op jit(solution)/shard_map/dot_general | solution.py:80
  71.2 0.3 fusion.26
  71.5 1.8 copy-done.1
  73.3 0.4 fusion.27
  74.0 1.6 copy.53
  75.6 1.3 mul.206
  76.8 3.1 %copy.50 = f32[2,256,768]{2,1,0:T(8,128)} copy(f32[2,256,768]{1,2,0:T(8,128)} %bitcast.80) | data formatting | bytes 3145728 | tf_op jit(solution)/shard_map/mul | solution.py:37
  79.9 1.6 copy.49
  81.5 4.8 %broadcast_select_fusion.3 = (bf16[2,256,768]{2,1,0:T(8,128)(2,1)}, bf16[2,256,768]{2,1,0:T(8,128)(2,1)}) fusion(bf16[2,256,768]{2,1,0:T(8,128)(2,1)} %param.22, pred[]{:T(512)S(6)} %eq.22, f32[2,256,768]{2,1,0:T(8,128)} %copy.53, f32[256,768]{1,0:T(8,128)} %copy.52, f32[256,768]{1,0:T(8,128)} %copy.51, f32[768]{0:T(1024)S(1)} %broadcast_bitcast_fusion, ...), kind=kLoop, calls=%fused_computation.54 | loop fusion | flops 2752512 | bytes 8653825 | tf_op jit(solution)/shard_map/jit(_where)/select_n | solution.py:120
  86.4 1.5 slice.60
  87.9 0.3 copy.58
  88.2 2.1 broadcast_select_fusion.2
  90.5 6.7 %all_gather.16 = bf16[2,128,768]{2,0,1:T(2,128)(2,1)} all-gather(bf16[2,32,768]{2,0,1:T(2,128)(2,1)S(1)} %copy.41), channel_id=1, replica_groups=mesh['batch'=4,'seq'=4,'head'=2] {'seq'}, dimensions={1}, use_global_device_ids=true | all-gather | bytes 491520 | tf_op jit(solution)/shard_map/all_gather | solution.py:98
  97.2 1.3 copy.42
  98.5 1.0 copy.45
  99.6 9.8 %all_gather.17 = bf16[2,128,768]{2,0,1:T(2,128)(2,1)} all-gather(bf16[2,32,768]{2,0,1:T(2,128)(2,1)S(1)} %copy.45), channel_id=1, replica_groups=mesh['batch'=4,'seq'=4,'head'=2] {'seq'}, dimensions={1}, use_global_device_ids=true | all-gather | bytes 491520 | tf_op jit(solution)/shard_map/all_gather | solution.py:99
  109.3 1.3 copy.46
  110.7 0.6 iota_compare_fusion.1
  111.3 1.2 copy.54
  112.7 0.4 fusion.23
  113.1 0.9 copy-done.3
  114.0 0.4 fusion.60
  114.4 0.2 fusion.36
  114.6 1.6 fusion.38
  116.2 0.6 all-gather.8.cloned.1.call-done
  116.9 3.2 %copy.55 = bf16[8,256,768]{1,2,0:T(8,128)(2,1)S(1)} copy(bf16[8,256,768]{2,1,0:T(8,128)(2,1)} %all-gather.8.cloned.1.call-done) | data formatting | bytes 6291456 | tf_op jit(solution)/shard_map/all_gather | solution.py:122
  120.0 26.9 %all-gather.10.cloned.1.call-done = bf16[8,256,768]{2,1,0:T(8,128)(2,1)} async-done(((bf16[2,256,768]{2,1,0:T(8,128)(2,1)}), bf16[8,256,768]{2,1,0:T(8,128)(2,1)}) %all-gather.10.cloned.1.call-update) | async-done | bytes 3145744 | tf_op jit(solution)/shard_map/all_gather | solution.py:123
  147.0 4.7 %copy.59 = bf16[8,256,768]{1,2,0:T(8,128)(2,1)} copy(bf16[8,256,768]{2,1,0:T(8,128)(2,1)} %all-gather.10.cloned.1.call-done) | data formatting | bytes 6291456 | tf_op jit(solution)/shard_map/all_gather | solution.py:123
  151.6 4.6 %broadcast_select_fusion.1 = (bf16[4,2,256,768]{2,3,1,0:T(8,128)(2,1)S(1)}, bf16[4,2,256,768]{2,3,1,0:T(8,128)(2,1)}) fusion(bf16[4,2,256,768]{2,3,1,0:T(8,128)(2,1)S(1)} %bitcast.75, pred[4]{0:T(512)(128)(4,1)S(1)} %copy-done.17, bf16[2,256,768]{1,2,0:T(8,128)(2,1)} %copy.54, bf16[4,2,256,768]{2,3,1,0:T(8,128)(2,1)} %bitcast.76, ...), kind=kLoop, calls=%fused_computation.27 | loop fusion | flops 3145728 | bytes 14155780 | tf_op jit(solution)/shard_map/jit(_where)/select_n | solution.py:126
  156.3 3.0 %multiply_reduce_fusion = (f32[2,6,256]{2,1,0:T(8,128)S(1)}, f32[2,6,256,4,256]{2,4,3,1,0:T(8,128)S(1)}) fusion(bf16[4,2,256,6,128]{2,4,3,1,0:T(8,128)(2,1)S(1)} %bitcast.74, bf16[2,256,6,128]{1,3,2,0:T(8,128)(2,1)} %copy-done.3), kind=kOutput, calls=%fused_computation.1 | convolution fusion | flops 811594752 | bytes 16527360 | tf_op jit(solution)/shard_map/pqhd,npkhd->phqnk/dot_general | solution.py:132
  159.3 2.1 fusion
  161.5 3.1 %copy-done = f32[2,6,256,4,256]{2,4,3,1,0:T(8,128)} copy-done((f32[2,6,256,4,256]{2,4,3,1,0:T(8,128)}, f32[2,6,256,4,256]{2,4,3,1,0:T(8,128)S(1)}, u32[]{:S(2)}) %copy-start) | copy-done | bytes 12582936
  164.6 11.3 %bitcast_convert_fusion = bf16[2,256,3072]{2,1,0:T(8,128)(2,1)} fusion(bf16[6,128,3072,1]{2,1,0,3:T(8,128)(2,1)} %bitcast.86, f32[2,6,256,128]{3,2,1,0:T(8,128)} %fusion.38, bf16[4,2,256,6,128]{2,4,3,1,0:T(8,128)(2,1)S(1)} %bitcast.83, f32[2,6,256,4,256]{2,4,3,1,0:T(8,128)} %copy-done, f32[2,6,256]{2,1,0:T(8,128)S(1)} %max.14, ...), kind=kOutput, calls=%fused_computation.13 | convolution fusion | flops 3233808384 | bytes 25202688 | tf_op jit(solution)/shard_map/phqd,hde->pqe/dot_general | solution.py:148
  176.0 43.5 %reduce-scatter.2.cloned.1.call-done = bf16[2,256,1536]{2,1,0:T(8,128)(2,1)} async-done(((bf16[2,256,3072]{2,1,0:T(8,128)(2,1)}), bf16[2,256,1536]{2,1,0:T(8,128)(2,1)}) %reduce-scatter.2.cloned.1.call-update) | async-done | bytes 1572880 | tf_op jit(solution)/shard_map/reduce_scatter | solution.py:154
  219.6 3.2 %add_convert_fusion = bf16[2,256,1536]{2,1,0:T(8,128)(2,1)} fusion(bf16[2,256,1536]{2,1,0:T(8,128)(2,1)S(1)} %copy-done.8, bf16[2,256,1536]{2,1,0:T(8,128)(2,1)} %reduce-scatter.2.cloned.1.call-done, bf16[2,256,1536]{2,1,0:T(8,128)(2,1)S(1)} %copy-done.5, f32[2,1536]{1,0:T(2,128)S(1)} %dynamic-slice_bitcast_fusion), kind=kLoop, calls=%fused_computation.21 | loop fusion | flops 5505024 | bytes 6303744 | tf_op jit(solution)/shard_map/convert_element_type | solution.py:163
  (67 shorter events, 1.1 us)
Async XLA Ops:
  6.5 50.0 %all-gather.6.cloned.1.call-start = ((), (), s32[]{:S(2)}) async-start(), calls=%async_computation.1 | async-start | bytes 4718592 | tf_op jit(solution)/shard_map/all_gather | solution.py:70
  7.3 109.6 %all-gather.8.cloned.1.call-start = ((), (), s32[]{:S(2)}) async-start(), calls=%async_computation.3 | async-start | bytes 3932160 | tf_op jit(solution)/shard_map/all_gather | solution.py:122
  7.3 18.8 %copy-start.18 = (s32[4]{0:T(128)S(1)}, s32[4]{0:T(128)}, u32[]{:S(2)}) copy-start(s32[4]{0:T(128)} %param.26) | copy-start | bytes 52
  7.3 18.8 %copy-start.19 = (s32[4]{0:T(128)S(1)}, s32[4]{0:T(128)}, u32[]{:S(2)}) copy-start(s32[4]{0:T(128)} %param.25) | copy-start | bytes 52
  26.1 6.2 %copy-start.16 = (f32[128]{0:T(128)S(1)}, f32[128]{0:T(128)}, u32[]{:S(2)}) copy-start(f32[128]{0:T(128)} %param.19) | copy-start | bytes 1540
  26.1 6.2 %copy-start.14 = (f32[2,3,3072]{2,0,1:T(2,128)S(1)}, f32[2,3,3072]{2,0,1:T(2,128)}, u32[]{:S(2)}) copy-start(f32[2,3,3072]{2,0,1:T(2,128)} %param.15) | copy-start | bytes 221188
  27.9 0.7 copy-start.9
  29.8 0.7 copy-start.11
  56.5 2.8 %copy-start.2 = (bf16[2,256,3072]{2,1,0:T(8,128)(2,1)S(1)}, bf16[2,256,3072]{2,1,0:T(8,128)(2,1)}, u32[]{:S(2)}) copy-start(bf16[2,256,3072]{2,1,0:T(8,128)(2,1)} %all-gather.6.cloned.1.call-done) | copy-start | bytes 9437188
  71.2 2.1 copy-start.1
  71.2 2.1 copy-start.20
  75.6 4.3 %slice-start = ((f32[2,256,3,6,128]{1,4,3,2,0:T(8,128)}), f32[2,256,1,6,128]{1,4,3,2,0:T(8,128)S(1)}, s32[]{:S(2)}) async-start(f32[2,256,3,6,128]{1,4,3,2,0:T(8,128)} %copy-done.1), calls=%async_computation.5 | async-start | bytes 3145728 | tf_op jit(solution)/shard_map/slice | solution.py:92
  86.3 4.1 %copy-start.13 = (bf16[2,32,768]{2,1,0:T(8,128)(2,1)S(1)}, bf16[2,32,768]{2,1,0:T(8,128)(2,1)}, u32[]{:S(2)}) copy-start(bf16[2,32,768]{2,1,0:T(8,128)(2,1)} %param.20) | copy-start | bytes 294916
  86.3 60.6 %all-gather.10.cloned.1.call-start = ((), (), s32[]{:S(2)}) async-start(), calls=%async_computation.4 | async-start | bytes 3932160 | tf_op jit(solution)/shard_map/all_gather | solution.py:123
  87.9 11.7 %copy-start.4 = (bf16[2,256,1,6,128]{1,4,3,2,0:T(8,128)(2,1)}, bf16[2,256,1,6,128]{1,4,3,2,0:T(8,128)(2,1)S(1)}, u32[]{:S(2)}) copy-start(bf16[2,256,1,6,128]{1,4,3,2,0:T(8,128)(2,1)S(1)} %slice.60) | copy-start | bytes 2359300
  88.2 23.1 %copy-start.21 = (s32[2]{0:T(128)S(1)}, s32[2]{0:T(128)}, u32[]{:S(2)}) copy-start(s32[2]{0:T(128)} %param.27) | copy-start | bytes 28
  90.3 21.0 %copy-start.7 = (bf16[2,256,768]{2,1,0:T(8,128)(2,1)S(1)}, bf16[2,256,768]{2,1,0:T(8,128)(2,1)}, u32[]{:S(2)}) copy-start(bf16[2,256,768]{2,1,0:T(8,128)(2,1)} %get-tuple-element.10) | copy-start | bytes 2359300
  90.3 129.2 %reduce-scatter.2.cloned.1.call-start = ((), (), s32[]{:S(2)}) async-start(), calls=%async_computation.2 | async-start | bytes 4718592 | tf_op jit(solution)/shard_map/reduce_scatter | solution.py:154
  109.3 3.3 %copy-start.10 = (f32[256,128]{0,1:T(8,128)S(1)}, f32[256,128]{0,1:T(8,128)}, u32[]{:S(2)}) copy-start(f32[256,128]{0,1:T(8,128)} %copy-done.9) | copy-start | bytes 393220
  109.3 3.4 %copy-start.12 = (f32[256,128]{0,1:T(8,128)S(1)}, f32[256,128]{0,1:T(8,128)}, u32[]{:S(2)}) copy-start(f32[256,128]{0,1:T(8,128)} %copy-done.11) | copy-start | bytes 393220
  113.1 0.9 copy-start.3
  120.0 31.6 %copy-start.17 = (pred[4]{0:T(512)(128)(4,1)S(1)}, pred[4]{0:T(512)(128)(4,1)}, u32[]{:S(2)}) copy-start(pred[4]{0:T(512)(128)(4,1)} %iota_compare_fusion.1) | copy-start | bytes 16
  159.3 5.3 %copy-start = (f32[2,6,256,4,256]{2,4,3,1,0:T(8,128)}, f32[2,6,256,4,256]{2,4,3,1,0:T(8,128)S(1)}, u32[]{:S(2)}) copy-start(f32[2,6,256,4,256]{2,4,3,1,0:T(8,128)S(1)} %get-tuple-element.28) | copy-start | bytes 37748740
  159.3 5.3 %copy-start.6 = (bf16[4,2,256,768]{2,3,1,0:T(8,128)(2,1)S(1)}, bf16[4,2,256,768]{2,3,1,0:T(8,128)(2,1)}, u32[]{:S(2)}) copy-start(bf16[4,2,256,768]{2,3,1,0:T(8,128)(2,1)} %get-tuple-element.24) | copy-start | bytes 9437188
  164.6 11.4 %copy-start.15 = (f32[2,1,3072]{2,0,1:T(2,128)S(1)}, f32[2,1,3072]{2,0,1:T(2,128)}, u32[]{:S(2)}) copy-start(f32[2,1,3072]{2,0,1:T(2,128)} %get-tuple-element.17) | copy-start | bytes 73732
  176.0 43.6 %copy-start.5 = (bf16[2,256,1536]{2,1,0:T(8,128)(2,1)S(1)}, bf16[2,256,1536]{2,1,0:T(8,128)(2,1)}, u32[]{:S(2)}) copy-start(bf16[2,256,1536]{2,1,0:T(8,128)(2,1)} %param.14) | copy-start | bytes 4718596
  176.0 43.6 %copy-start.8 = (bf16[2,256,1536]{2,1,0:T(8,128)(2,1)S(1)}, bf16[2,256,1536]{2,1,0:T(8,128)(2,1)}, u32[]{:S(2)}) copy-start(bf16[2,256,1536]{2,1,0:T(8,128)(2,1)} %param.24) | copy-start | bytes 4718596
Sparse Core Ops, SparseCore 0:
  8.9 47.6 all-gather.5
  86.4 30.3 all-gather.7
  118.4 28.4 all-gather.9
  176.1 43.3 reduce-scatter.1
where the time goes:
time: 230 us; the launch traced here: 229 us
  waiting for transfers between devices  95.4 us (41%)
  local copies, waits for them, and re-layouts  51.2 us (22%)
  matrix products  27.2 us (12%)
  other arithmetic  24.2 us (11%)
  blocking collectives  16.5 us (7%)
  between operations  14.8 us (6%)
    reduce_scatter x1, waiting for transfers between devices, per_device(): lax.psum_scatter(partial_value.astype(jnp.bfloat16), 'head', scatter_dime...  43.5 us
    unnamed x47, local copies, waits for them, and re-layouts  27.4 us
    all_gather x1, waiting for transfers between devices, per_device(): value_rows = lax.all_gather(chosen_v[None], 'seq', axis=0, tiled=True)  26.9 us
    all_gather x1, waiting for transfers between devices, per_device(): gathered = lax.all_gather(image_hidden, 'head', axis=2, tiled=True)  23.5 us
    dot_general x1, matrix products, per_device(): jnp.einsum('phqd,hde->pqe', attended, out_weight.reshape(local_heads, hea...  11.3 us
    dot_general x1, matrix products, per_device(): jnp.dot(modulated.reshape(prompts * tok_rows, model_width), qkv_weight.re...  10.8 us
    all_gather x1, blocking collectives, per_device(): lax.all_gather(text_values, 'seq', axis=1, tiled=True)  9.76 us
    all_gather x1, blocking collectives, per_device(): lax.all_gather(text_keys, 'seq', axis=1, tiled=True)  6.72 us
  transfers between devices with their start and end apart: 4, of which 4 were waited for; matrix products, arithmetic and copies ran while one was open for 17% of the time, Pallas kernels for 0%

commit v1 on v0

--- a/solution.py
+++ b/solution.py
@@ -5,6 +5,16 @@
 
 GRID_W = 64
 epsilon = 1e-06
+
+
+def ring_gather(x, axis, dim):
+    ways, here, step = (lax.axis_size(axis), lax.axis_index(axis), x.shape[dim])
+    lengths = [n * ways if d == dim else n for d, n in enumerate(x.shape)]
+    full = lax.dynamic_update_slice_in_dim(jnp.zeros(lengths, x.dtype), x, here * step, axis=dim)
+    for far in range(1, ways):
+        x = lax.ppermute(x, axis, [(d, (d + 1) % ways) for d in range(ways)])
+        full = lax.dynamic_update_slice_in_dim(full, x, (here - far) % ways * step, axis=dim)
+    return full
 
 
 def rotary_tables(raster, head_dim, grid_width):
@@ -96,7 +106,7 @@
     score_scale = head_dim ** (-0.5)
     text_k, text_v = (
         lax.all_gather(text_keys, "seq", axis=1, tiled=True),
-        lax.all_gather(text_values, "seq", axis=1, tiled=True),
+        ring_gather(text_values, "seq", 1),
     )
     total_text = text_k.shape[1]
     text_key_rows = text_k.reshape(prompts, total_text, local_heads, head_dim)

time: 230 us -> 246 us (1.070)
  local copies, waits for them, and re-layouts: 51.2 us -> 77.8 us
  waiting for transfers between devices: 95.4 us -> 78 us
  blocking collectives: 16.5 us -> 19.2 us
    all_gather x1, waiting for transfers between devices: 26.9 us -> 0.01 us  [per_device(): value_rows = lax.all_gather(chosen_v[None], 'seq', axis=0, tiled=True)]
    dynamic_update_slice x0 -> x4, local copies, waits for them, and re-layouts: none -> 24 us  [the longest x3 18.8 us: ring_gather(): lax.dynamic_update_slice_in_dim(full, x, (here - far) % ways * step, axis...]
    all_gather x1, blocking collectives: 6.72 us -> 19.2 us  [per_device(): lax.all_gather(text_keys, 'seq', axis=1, tiled=True)]
    ppermute x0 -> x3, waiting for transfers between devices: none -> 10.5 us  [ring_gather(): x = lax.ppermute(x, axis, [(d, (d + 1) % ways) for d in range(ways)])]
    all_gather x1 -> x0, blocking collectives: 9.76 us -> none  [per_device(): lax.all_gather(text_values, 'seq', axis=1, tiled=True)]
    dot_general x1, matrix products: 1.59 us -> 6.27 us  [per_device(): jnp.einsum('phqnk,npkhd->phqd', weights.astype(jnp.bfloat16), value_rows,...]
    dot_general x1, matrix products: 11.3 us -> 7.14 us  [per_device(): jnp.einsum('phqd,hde->pqe', attended, out_weight.reshape(local_heads, hea...]
    unnamed x47 -> x55, local copies, waits for them, and re-layouts: 27.4 us -> 28.9 us
  transfers between devices with their start and end apart: 4 -> 7, of which waited for: 4 -> 3; matrix products, arithmetic and copies ran while one was open for 17% -> 26% of each run, Pallas kernels for 0% -> 0%
where the time goes in v1:
time: 246 us; the launch traced here: 244 us
  waiting for transfers between devices  78 us (32%)
  local copies, waits for them, and re-layouts  77.8 us (32%)
  matrix products  27.7 us (11%)
  other arithmetic  25.1 us (10%)
  blocking collectives  19.2 us (8%)
  between operations  15 us (6%)
    reduce_scatter x1, waiting for transfers between devices, per_device(): lax.psum_scatter(partial_value.astype(jnp.bfloat16), 'head', scatter_dime...  43.2 us
    unnamed x55, local copies, waits for them, and re-layouts  28.9 us
    all_gather x1, waiting for transfers between devices, per_device(): gathered = lax.all_gather(image_hidden, 'head', axis=2, tiled=True)  23.6 us
    all_gather x1, blocking collectives, per_device(): lax.all_gather(text_keys, 'seq', axis=1, tiled=True)  19.2 us
    dynamic_update_slice x3, local copies, waits for them, and re-layouts, ring_gather(): lax.dynamic_update_slice_in_dim(full, x, (here - far) % ways * step, axis...  18.8 us
    dot_general x1, matrix products, per_device(): jnp.dot(modulated.reshape(prompts * tok_rows, model_width), qkv_weight.re...  10.8 us
    ppermute x3, waiting for transfers between devices, ring_gather(): x = lax.ppermute(x, axis, [(d, (d + 1) % ways) for d in range(ways)])  10.5 us
    dot_general x1, matrix products, per_device(): jnp.einsum('phqd,hde->pqe', attended, out_weight.reshape(local_heads, hea...  7.14 us
  transfers between devices with their start and end apart: 7, of which 3 were waited for; matrix products, arithmetic and copies ran while one was open for 26% of the time, Pallas kernels for 0%

profile of v1, /device:TPU:0, one launch (start us, length us, event | category | flops | bytes accessed | tf_op | source)
XLA Modules:
  0.0 244.3 jit_solution(16612939220886836626)
XLA Ops:
  6.5 0.7 all-gather.6.cloned.1.call-update
  7.3 18.8 %copy.41 = bf16[3072,3,768]{0,2,1:T(8,128)(2,1)} copy(bf16[3072,3,768]{2,0,1:T(8,128)(2,1)} %param.16) | data formatting | bytes 28311552 | tf_op args[2]
  26.1 0.7 select_reduce_fusion
  27.9 0.6 copy-done.11
  28.6 1.2 copy.53
  29.8 0.6 copy-done.13
  30.5 1.1 copy.52
  32.4 0.6 fusion.51
  33.0 23.6 %all-gather.6.cloned.1.call-done = bf16[2,256,3072]{2,1,0:T(8,128)(2,1)} async-done(((bf16[2,256,1536]{2,1,0:T(8,128)(2,1)}), bf16[2,256,3072]{2,1,0:T(8,128)(2,1)}) %all-gather.6.cloned.1.call-update) | async-done | bytes 3145744 | tf_op jit(solution)/shard_map/all_gather | solution.py:80
  56.5 2.5 %convert_reduce_fusion = f32[2,256]{1,0:T(2,128)S(1)} fusion(bf16[2,256,3072]{2,1,0:T(8,128)(2,1)} %all-gather.6.cloned.1.call-done), kind=kLoop, calls=%fused_computation.5 | loop fusion | flops 3145216 | bytes 3147776 | tf_op jit(solution)/shard_map/reduce_sum | solution.py:83
  59.4 1.0 fusion.4
  60.3 10.8 %fusion.13 = f32[2,256,3,6,128]{1,4,3,2,0:T(8,128)S(1)} fusion(bf16[3,6,128,3072,1]{3,2,1,0,4:T(8,128)(2,1)} %bitcast.73, bf16[2,256,3072]{2,1,0:T(8,128)(2,1)S(1)} %copy-done.2, f32[2,3072]{1,0:T(2,128)S(1)} %get-tuple-element.18, f32[2,3072]{1,0:T(2,128)S(1)} %get-tuple-element.19, f32[2,256]{1,0:T(2,128)S(1)} %add_rsqrt_fusion.2, ...), kind=kOutput, calls=%fused_computation.17 | convolution fusion | flops 7257194496 | bytes 22073344 | tf_op jit(solution)/shard_map/dot_general | solution.py:90
  71.5 1.8 copy-done.1
  74.0 1.6 copy.54
  75.6 1.3 mul.222
  76.8 3.1 %copy.51 = f32[2,256,768]{2,1,0:T(8,128)} copy(f32[2,256,768]{1,2,0:T(8,128)} %bitcast.81) | data formatting | bytes 3145728 | tf_op jit(solution)/shard_map/mul | solution.py:47
  79.9 1.6 copy.50
  81.5 4.8 %broadcast_select_fusion.3 = (bf16[2,256,768]{2,1,0:T(8,128)(2,1)}, bf16[2,256,768]{2,1,0:T(8,128)(2,1)}) fusion(bf16[2,256,768]{2,1,0:T(8,128)(2,1)} %param.22, pred[]{:T(512)S(6)} %eq.26, f32[2,256,768]{2,1,0:T(8,128)} %copy.54, f32[256,768]{1,0:T(8,128)} %copy.53, f32[256,768]{1,0:T(8,128)} %copy.52, f32[768]{0:T(1024)S(1)} %broadcast_bitcast_fusion, ...), kind=kLoop, calls=%fused_computation.53 | loop fusion | flops 2752512 | bytes 8653825 | tf_op jit(solution)/shard_map/jit(_where)/select_n | solution.py:130
  86.4 1.5 slice.60
  88.2 2.1 broadcast_select_fusion.2
  90.4 1.2 copy.46
  91.6 0.6 iota_compare_fusion
  92.2 1.0 copy.42
  93.3 10.5 %collective-permute-done = bf16[2,32,768]{1,2,0:T(8,128)(2,1)} collective-permute-done((bf16[2,32,768]{1,2,0:T(8,128)(2,1)S(1)}, bf16[2,32,768]{1,2,0:T(8,128)(2,1)}, u32[]{:S(2)}, u32[]{:S(2)}) %collective-permute-start) | collective-permute-done | bytes 98336 | tf_op jit(solution)/shard_map/ppermute | solution.py:15
  103.7 19.2 %all_gather.13 = bf16[2,128,768]{2,0,1:T(2,128)(2,1)} all-gather(bf16[2,32,768]{2,0,1:T(2,128)(2,1)S(1)} %copy.42), channel_id=1, replica_groups=mesh['batch'=4,'seq'=4,'head'=2] {'seq'}, dimensions={1}, use_global_device_ids=true | all-gather | bytes 491520 | tf_op jit(solution)/shard_map/all_gather | solution.py:108
  122.9 1.3 copy.43
  124.3 5.2 %dynamic_update_slice.12 = bf16[2,128,768]{1,2,0:T(8,128)(2,1)S(1)} dynamic-update-slice(bf16[2,128,768]{1,2,0:T(8,128)(2,1)S(1)} %broadcast_in_dim.109, bf16[2,32,768]{1,2,0:T(8,128)(2,1)} %copy-done.10, s32[]{:T(128)} %constant.84.clone.1, s32[]{:T(128)S(6)} %select_n.107, s32[]{:T(128)} %constant.84.clone.1) | dynamic-update-slice | bytes 196612 | tf_op jit(solution)/shard_map/dynamic_update_slice | solution.py:13
  129.6 1.4 collective-permute-start.2
  131.0 0.6 iota_compare_fusion.1
  131.6 6.2 %dynamic_update_slice.13 = bf16[2,128,768]{1,2,0:T(8,128)(2,1)S(1)} dynamic-update-slice(bf16[2,128,768]{1,2,0:T(8,128)(2,1)S(1)} %dynamic_update_slice.12, bf16[2,32,768]{1,2,0:T(8,128)(2,1)} %collective-permute-done, s32[]{:T(128)} %constant.84.clone.1, s32[]{:T(128)S(6)} %select_n.109, s32[]{:T(128)} %constant.84.clone.1) | dynamic-update-slice | bytes 196612 | tf_op jit(solution)/shard_map/dynamic_update_slice | solution.py:16
  137.8 6.3 %dynamic_update_slice.14 = bf16[2,128,768]{1,2,0:T(8,128)(2,1)S(1)} dynamic-update-slice(bf16[2,128,768]{1,2,0:T(8,128)(2,1)S(1)} %dynamic_update_slice.13, bf16[2,32,768]{1,2,0:T(8,128)(2,1)} %collective-permute-done.1, s32[]{:T(128)} %constant.84.clone.1, s32[]{:T(128)S(6)} %select_n.111, s32[]{:T(128)} %constant.84.clone.1) | dynamic-update-slice | bytes 196612 | tf_op jit(solution)/shard_map/dynamic_update_slice | solution.py:16
  144.2 6.3 %dynamic_update_slice.15 = bf16[2,128,768]{1,2,0:T(8,128)(2,1)S(1)} dynamic-update-slice(bf16[2,128,768]{1,2,0:T(8,128)(2,1)S(1)} %dynamic_update_slice.14, bf16[2,32,768]{1,2,0:T(8,128)(2,1)} %collective-permute-done.2, s32[]{:T(128)} %constant.84.clone.1, s32[]{:T(128)S(6)} %select_n.113, s32[]{:T(128)} %constant.84.clone.1) | dynamic-update-slice | bytes 196612 | tf_op jit(solution)/shard_map/dynamic_update_slice | solution.py:16
  150.5 1.2 copy.55
  152.2 0.9 copy-done.3
  153.6 1.1 copy-done.5
  154.7 0.8 fusion.28
  155.6 4.7 %copy.56 = bf16[8,256,768]{1,2,0:T(8,128)(2,1)} copy(bf16[8,256,768]{2,1,0:T(8,128)(2,1)} %all-gather.8.cloned.1.call-done) | data formatting | bytes 6291456 | tf_op jit(solution)/shard_map/all_gather | solution.py:132
  160.3 4.7 %copy.60 = bf16[8,256,768]{1,2,0:T(8,128)(2,1)} copy(bf16[8,256,768]{2,1,0:T(8,128)(2,1)} %all-gather.10.cloned.1.call-done) | data formatting | bytes 6291456 | tf_op jit(solution)/shard_map/all_gather | solution.py:133
  164.9 3.9 %broadcast_select_fusion = (bf16[4,2,256,768]{2,3,1,0:T(8,128)(2,1)S(1)}, bf16[4,2,256,768]{2,3,1,0:T(8,128)(2,1)S(1)}) fusion(bf16[4,2,256,768]{2,3,1,0:T(8,128)(2,1)} %bitcast.77, pred[4]{0:T(512)(128)(4,1)S(1)} %copy-done.21, bf16[2,256,768]{1,2,0:T(8,128)(2,1)} %bitcast.79, bf16[4,2,256,768]{2,3,1,0:T(8,128)(2,1)} %bitcast.76, bf16[2,256,768]{1,2,0:T(8,128)(2,1)} %copy.55), kind=kLoop, calls=%fused_computation.26 | loop fusion | flops 3145728 | bytes 14155780 | tf_op jit(solution)/shard_map/jit(_where)/select_n | solution.py:137
  168.9 3.0 %multiply_reduce_fusion = (f32[2,6,256]{2,1,0:T(8,128)S(1)}, f32[2,6,256,4,256]{2,4,3,1,0:T(8,128)S(1)}) fusion(bf16[4,2,256,6,128]{2,4,3,1,0:T(8,128)(2,1)S(1)} %bitcast.75, bf16[2,256,6,128]{1,3,2,0:T(8,128)(2,1)} %copy-done.3), kind=kOutput, calls=%fused_computation.1 | convolution fusion | flops 811594752 | bytes 16527360 | tf_op jit(solution)/shard_map/pqhd,npkhd->phqnk/dot_general | solution.py:142
  171.9 2.1 fusion
  173.9 2.4 copy-done
  176.4 6.3 %fusion.8 = f32[2,6,256,128,1]{3,2,4,1,0:T(8,128)S(1)} fusion(f32[2,6,256,4,256]{2,4,3,1,0:T(8,128)} %copy-done, f32[2,6,256]{2,1,0:T(8,128)S(1)} %max.14, bf16[4,2,256,6,128]{2,4,3,1,0:T(8,128)(2,1)S(1)} %bitcast.74), kind=kOutput, calls=%fused_computation.12 | convolution fusion | flops 814743552 | bytes 17313792 | tf_op jit(solution)/shard_map/phqnk,npkhd->phqd/dot_general | solution.py:149
  182.7 0.6 multiply_add_fusion
  183.3 7.1 %bitcast_convert_fusion = bf16[2,256,3072]{2,1,0:T(8,128)(2,1)} fusion(bf16[6,128,3072,1]{2,1,0,3:T(8,128)(2,1)} %bitcast.86, f32[2,6,256,128,1]{3,2,4,1,0:T(8,128)S(1)} %fusion.8, bf16[2,128,6,128]{1,3,2,0:T(8,128)(2,1)S(1)} %bitcast.85, f32[2,6,256,128]{2,3,1,0:T(8,128)S(1)} %copy-done.6, f32[2,6,256]{2,1,0:T(8,128)} %get-tuple-element.7, ...), kind=kOutput, calls=%fused_computation.13 | convolution fusion | flops 2520514560 | bytes 11440128 | tf_op jit(solution)/shard_map/phqd,hde->pqe/dot_general | solution.py:158
  190.5 0.9 dynamic-slice_bitcast_fusion
  191.3 43.2 %reduce-scatter.2.cloned.1.call-done = bf16[2,256,1536]{2,1,0:T(8,128)(2,1)} async-done(((bf16[2,256,3072]{2,1,0:T(8,128)(2,1)}), bf16[2,256,1536]{2,1,0:T(8,128)(2,1)}) %reduce-scatter.2.cloned.1.call-update) | async-done | bytes 1572880 | tf_op jit(solution)/shard_map/reduce_scatter | solution.py:164
  234.6 3.2 %add_convert_fusion = bf16[2,256,1536]{2,1,0:T(8,128)(2,1)} fusion(bf16[2,256,1536]{2,1,0:T(8,128)(2,1)S(1)} %copy-done.9, bf16[2,256,1536]{2,1,0:T(8,128)(2,1)} %reduce-scatter.2.cloned.1.call-done, bf16[2,256,1536]{2,1,0:T(8,128)(2,1)S(1)} %copy-done.7, f32[2,1536]{1,0:T(2,128)S(1)} %dynamic-slice_bitcast_fusion), kind=kLoop, calls=%fused_computation.21 | loop fusion | flops 5505024 | bytes 6303744 | tf_op jit(solution)/shard_map/convert_element_type | solution.py:173
  (84 shorter events, 3.4 us)
Async XLA Ops:
  6.5 50.0 %all-gather.6.cloned.1.call-start = ((), (), s32[]{:S(2)}) async-start(), calls=%async_computation.1 | async-start | bytes 4718592 | tf_op jit(solution)/shard_map/all_gather | solution.py:80
  7.3 148.3 %all-gather.8.cloned.1.call-start = ((), (), s32[]{:S(2)}) async-start(), calls=%async_computation.3 | async-start | bytes 3932160 | tf_op jit(solution)/shard_map/all_gather | solution.py:132
  7.3 18.8 %copy-start.22 = (s32[4]{0:T(128)S(1)}, s32[4]{0:T(128)}, u32[]{:S(2)}) copy-start(s32[4]{0:T(128)} %param.26) | copy-start | bytes 52
  7.3 18.8 %copy-start.23 = (s32[4]{0:T(128)S(1)}, s32[4]{0:T(128)}, u32[]{:S(2)}) copy-start(s32[4]{0:T(128)} %param.25) | copy-start | bytes 52
  26.1 6.2 %copy-start.19 = (f32[128]{0:T(128)S(1)}, f32[128]{0:T(128)}, u32[]{:S(2)}) copy-start(f32[128]{0:T(128)} %param.19) | copy-start | bytes 1540
  26.1 6.2 %copy-start.17 = (f32[2,3,3072]{2,0,1:T(2,128)S(1)}, f32[2,3,3072]{2,0,1:T(2,128)}, u32[]{:S(2)}) copy-start(f32[2,3,3072]{2,0,1:T(2,128)} %param.15) | copy-start | bytes 221188
  27.9 0.7 copy-start.11
  29.8 0.6 copy-start.13
  56.5 2.8 %copy-start.2 = (bf16[2,256,3072]{2,1,0:T(8,128)(2,1)S(1)}, bf16[2,256,3072]{2,1,0:T(8,128)(2,1)}, u32[]{:S(2)}) copy-start(bf16[2,256,3072]{2,1,0:T(8,128)(2,1)} %all-gather.6.cloned.1.call-done) | copy-start | bytes 9437188
  71.2 2.1 copy-start.1
  71.2 2.1 copy-start.24
  75.6 4.3 %slice-start = ((f32[2,256,3,6,128]{1,4,3,2,0:T(8,128)}), f32[2,256,1,6,128]{1,4,3,2,0:T(8,128)S(1)}, s32[]{:S(2)}) async-start(f32[2,256,3,6,128]{1,4,3,2,0:T(8,128)} %copy-done.1), calls=%async_computation.5 | async-start | bytes 3145728 | tf_op jit(solution)/shard_map/slice | solution.py:102
  86.3 5.3 %copy-start.25 = (s32[2]{0:T(128)S(1)}, s32[2]{0:T(128)}, u32[]{:S(2)}) copy-start(s32[2]{0:T(128)} %param.27) | copy-start | bytes 28
  86.3 74.0 %all-gather.10.cloned.1.call-start = ((), (), s32[]{:S(2)}) async-start(), calls=%async_computation.4 | async-start | bytes 3932160 | tf_op jit(solution)/shard_map/all_gather | solution.py:133
  87.9 36.4 %copy-start.4 = (bf16[2,256,1,6,128]{1,4,3,2,0:T(8,128)(2,1)}, bf16[2,256,1,6,128]{1,4,3,2,0:T(8,128)(2,1)S(1)}, u32[]{:S(2)}) copy-start(bf16[2,256,1,6,128]{1,4,3,2,0:T(8,128)(2,1)S(1)} %slice.60) | copy-start | bytes 2359300
  90.3 60.2 %copy-start.8 = (bf16[2,256,768]{2,1,0:T(8,128)(2,1)S(1)}, bf16[2,256,768]{2,1,0:T(8,128)(2,1)}, u32[]{:S(2)}) copy-start(bf16[2,256,768]{2,1,0:T(8,128)(2,1)} %get-tuple-element.10) | copy-start | bytes 2359300
  90.3 144.3 %reduce-scatter.2.cloned.1.call-start = ((), (), s32[]{:S(2)}) async-start(), calls=%async_computation.2 | async-start | bytes 4718592 | tf_op jit(solution)/shard_map/reduce_scatter | solution.py:164
  91.5 12.2 %copy-start.10 = (bf16[2,32,768]{1,2,0:T(8,128)(2,1)}, bf16[2,32,768]{1,2,0:T(8,128)(2,1)S(1)}, u32[]{:S(2)}) copy-start(bf16[2,32,768]{1,2,0:T(8,128)(2,1)S(1)} %copy.46) | copy-start | bytes 294916
  91.5 12.2 %collective-permute-start = (bf16[2,32,768]{1,2,0:T(8,128)(2,1)S(1)}, bf16[2,32,768]{1,2,0:T(8,128)(2,1)}, u32[]{:S(2)}, u32[]{:S(2)}) collective-permute-start(bf16[2,32,768]{1,2,0:T(8,128)(2,1)S(1)} %copy.46), channel_id=1, source_target_pairs={{0,2},{2,4},{4,6},{6,0},{1,3},{3,5},{5,7},{7,1},{8,10},{10,12},{12... | collective-permute-start | bytes 294920 | tf_op jit(solution)/shard_map/ppermute | solution.py:15
  103.7 25.8 %collective-permute-start.1 = (bf16[2,32,768]{1,2,0:T(8,128)(2,1)}, bf16[2,32,768]{1,2,0:T(8,128)(2,1)}, u32[]{:S(2)}, u32[]{:S(2)}) collective-permute-start(bf16[2,32,768]{1,2,0:T(8,128)(2,1)} %collective-permute-done), channel_id=1, source_target_pairs={{0,2},{2,4},{4,6},{6,0},{1,3},{3,5},{5,7},{7,1},{8,10},{10,12},{12... | collective-permute-start | bytes 294920 | tf_op jit(solution)/shard_map/ppermute | solution.py:15
  129.6 14.6 %collective-permute-start.2 = (bf16[2,32,768]{1,2,0:T(8,128)(2,1)}, bf16[2,32,768]{1,2,0:T(8,128)(2,1)}, u32[]{:S(2)}, u32[]{:S(2)}) collective-permute-start(bf16[2,32,768]{1,2,0:T(8,128)(2,1)} %collective-permute-done.1), channel_id=1, source_target_pairs={{0,2},{2,4},{4,6},{6,0},{1,3},{3,5},{5,7},{7,1},{8,10},{10,12},{12... | collective-permute-start | bytes 294920 | tf_op jit(solution)/shard_map/ppermute | solution.py:15
  137.8 14.0 %copy-start.12 = (f32[256,128]{0,1:T(8,128)S(1)}, f32[256,128]{0,1:T(8,128)}, u32[]{:S(2)}) copy-start(f32[256,128]{0,1:T(8,128)} %copy-done.11) | copy-start | bytes 393220
  137.8 14.0 %copy-start.14 = (f32[256,128]{0,1:T(8,128)S(1)}, f32[256,128]{0,1:T(8,128)}, u32[]{:S(2)}) copy-start(f32[256,128]{0,1:T(8,128)} %copy-done.13) | copy-start | bytes 393220
  150.4 1.8 copy-start.15
  151.6 1.5 copy-start.20
  152.2 0.9 copy-start.3
  153.6 1.1 copy-start.5
  160.3 4.7 %copy-start.21 = (pred[4]{0:T(512)(128)(4,1)S(1)}, pred[4]{0:T(512)(128)(4,1)}, u32[]{:S(2)}) copy-start(pred[4]{0:T(512)(128)(4,1)} %iota_compare_fusion.1) | copy-start | bytes 16
  171.9 4.5 %copy-start = (f32[2,6,256,4,256]{2,4,3,1,0:T(8,128)}, f32[2,6,256,4,256]{2,4,3,1,0:T(8,128)S(1)}, u32[]{:S(2)}) copy-start(f32[2,6,256,4,256]{2,4,3,1,0:T(8,128)S(1)} %get-tuple-element.28) | copy-start | bytes 37748740
  176.4 6.3 %copy-start.18 = (f32[2,6,256]{2,1,0:T(8,128)S(1)}, f32[2,6,256]{2,1,0:T(8,128)}, u32[]{:S(2)}) copy-start(f32[2,6,256]{2,1,0:T(8,128)} %fusion.28) | copy-start | bytes 36868
  176.4 6.9 %copy-start.6 = (f32[2,6,256,128]{2,3,1,0:T(8,128)S(1)}, f32[2,6,256,128]{2,3,1,0:T(8,128)}, u32[]{:S(2)}) copy-start(f32[2,6,256,128]{2,3,1,0:T(8,128)} %copy-done.5) | copy-start | bytes 4718596
  176.4 6.9 %copy-start.16 = (bf16[2,128,768]{1,2,0:T(8,128)(2,1)S(1)}, bf16[2,128,768]{1,2,0:T(8,128)(2,1)}, u32[]{:S(2)}) copy-start(bf16[2,128,768]{1,2,0:T(8,128)(2,1)} %copy-done.15) | copy-start | bytes 1179652
  190.4 44.1 %copy-start.7 = (bf16[2,256,1536]{2,1,0:T(8,128)(2,1)S(1)}, bf16[2,256,1536]{2,1,0:T(8,128)(2,1)}, u32[]{:S(2)}) copy-start(bf16[2,256,1536]{2,1,0:T(8,128)(2,1)} %param.14) | copy-start | bytes 4718596
  190.4 44.1 %copy-start.9 = (bf16[2,256,1536]{2,1,0:T(8,128)(2,1)S(1)}, bf16[2,256,1536]{2,1,0:T(8,128)(2,1)}, u32[]{:S(2)}) copy-start(bf16[2,256,1536]{2,1,0:T(8,128)(2,1)} %param.24) | copy-start | bytes 4718596
Sparse Core Ops, SparseCore 0:
  8.9 47.6 all-gather.5
  86.4 36.1 all-gather.7
  124.2 31.3 all-gather.9
  190.6 43.9 reduce-scatter.1
